TPU v7x, 32 devices: a whole 2x2x4 slice. The times are simulated.
32 devices in a mesh: row: 2 (over x), col: 16 (over z, y, core).
Axes of the slice: x: 2, y: 2, z: 4, core: 2. Of those that a mesh axis runs over, the one named last changes fastest.
Arguments:
- tokens: bfloat16 [512, 4608], P('col', 'row'), may hold values from -6 to 6
- pre_gain: float32 [2, 4608], P(None, 'row'), may hold values from -0.6 to 0.6
- post_gain: float32 [2, 4608], P(None, 'row'), may hold values from -0.6 to 0.6
- gate_weight: bfloat16 [2, 4608, 36864], P(None, ('row', 'col')), may hold values from -0.09375 to 0.09375
- up_weight: bfloat16 [2, 4608, 36864], P(None, ('row', 'col')), may hold values from -0.09375 to 0.09375
- down_weight: bfloat16 [2, 36864, 4608], P(None, ('row', 'col')), may hold values from -0.13541667 to 0.13541667
Outputs:
- stream: bfloat16 [512, 4608], P('col', 'row')
All inputs are finite; a program needn't handle non-finite values.
Results may differ from a plain program's by a relative error of at most 0.019.
Values may be sent and summed in bfloat16 or wider, within the bound.
A program may use at most 256 MiB of HBM per device.

v0:
```python
import jax
import jax.numpy as jnp
from jax import lax
from jax.sharding import PartitionSpec as P

norm_eps = 1e-06


def activate(summed, columns):
    gate = summed[:, :columns]
    up_proj = summed[:, columns:]
    return (jax.nn.gelu(gate, approximate=True) * up_proj).astype(jnp.bfloat16)


def on_device(tokens, pre_gain, post_gain, gate_weight, up_weight, down_weight):
    layer_count = gate_weight.shape[0]
    row_count = lax.axis_size("row")
    col_count = lax.axis_size("col")
    model_width = tokens.shape[1] * row_count
    stored_rows = gate_weight.shape[1]
    hidden_total = gate_weight.shape[2]
    block_width = hidden_total // (row_count * col_count)
    tile_rows = stored_rows * col_count
    tile_columns = hidden_total // col_count
    current = tokens
    for layer_index in range(layer_count):
        gate_split = gate_weight[layer_index].reshape(
            stored_rows, row_count, col_count, block_width
        )
        up_split = up_weight[layer_index].reshape(stored_rows, row_count, col_count, block_width)
        gate_tile, up_tile = (
            lax.all_to_all(gate_split, "col", split_axis=2, concat_axis=0, tiled=True),
            lax.all_to_all(up_split, "col", split_axis=2, concat_axis=0, tiled=True),
        )
        gate_up = jnp.concatenate(
            (gate_tile.reshape(tile_rows, tile_columns), up_tile.reshape(tile_rows, tile_columns)),
            axis=1,
        )
        down_tile = lax.all_to_all(
            down_weight[layer_index], "row", split_axis=1, concat_axis=0, tiled=True
        )
        columns = gate_up.shape[1] // 2
        values = current.astype(jnp.float32)
        squares = lax.psum(jnp.sum(values * values, axis=1), "row")
        scale_pre = lax.rsqrt(squares / model_width + norm_eps)[:, None]
        normed = (values * scale_pre * (1.0 + pre_gain[layer_index])[None, :]).astype(jnp.bfloat16)
        partial_sums = jnp.dot(
            lax.all_gather(normed, "col", axis=0, tiled=True),
            gate_up,
            preferred_element_type=jnp.float32,
        )
        summed = lax.psum(partial_sums.astype(jnp.bfloat16), "row").astype(jnp.float32)
        hidden = activate(summed, columns)
        branch = lax.psum_scatter(
            jnp.dot(hidden, down_tile, preferred_element_type=jnp.float32),
            "col",
            scatter_dimension=0,
            tiled=True,
        )
        branch_squares = lax.psum(jnp.sum(branch * branch, axis=1), "row")
        scale_post = lax.rsqrt(branch_squares / model_width + norm_eps)[:, None]
        post = branch * scale_post * (1.0 + post_gain[layer_index])[None, :]
        current = (values + post).astype(jnp.bfloat16)
    return current


def solution(mesh):
    in_specs = (
        P("col", "row"),
        P(None, "row"),
        P(None, "row"),
        P(None, ("row", "col"), None),
        P(None, ("row", "col"), None),
        P(None, ("row", "col"), None),
    )
    out_specs = P("col", "row")
    return jax.shard_map(
        on_device, mesh=mesh, in_specs=in_specs, out_specs=out_specs, check_vma=False
    )
```

profile of v0, /device:TPU:0, one launch (start us, length us, event | category | flops | bytes accessed | tf_op | source)
XLA Modules:
  0.0 1513.6 jit_solution(6877893643753962465)
XLA Ops:
  6.5 15.8 %fusion.65 = (bf16[1,1152,4608]{2,1,0:T(8,128)(2,1)}, bf16[1,1152,4608]{2,1,0:T(8,128)(2,1)}) fusion(bf16[2,1152,4608]{2,1,0:T(8,128)(2,1)} %param.11), kind=kLoop, calls=%fused_computation.76 | loop fusion | bytes 42467328 | tf_op jit(solution)/shard_map/slice | solution.py:40
  22.3 15.2 %copy.19 = bf16[1,1152,4608]{1,2,0:T(8,128)(2,1)} copy(bf16[1,1152,4608]{2,1,0:T(8,128)(2,1)} %get-tuple-element.16) | data formatting | bytes 21233664
  37.6 7.8 all-to-all-start.2
  45.4 12.6 fusion.63
  58.0 3.7 copy.21
  61.7 15.8 %copy.11 = bf16[144,2,16,1152]{3,1,0,2:T(2,128)(2,1)} copy(bf16[144,2,16,1152]{3,2,1,0:T(8,128)(2,1)S(1)} %bitcast.56) | data formatting | bytes 21233664 | tf_op jit(solution)/shard_map/reshape;squeeze | solution.py:27
  77.5 85.5 %all-to-all-done.2 = bf16[1152,2,2304]{0,2,1:T(8,128)(2,1)} async-done(((bf16[1152,2,2304]{0,2,1:T(8,128)(2,1)}), bf16[1152,2,2304]{0,2,1:T(8,128)(2,1)}, u32[]{:S(2)}, u32[]{:S(2)}) %all-to-all-start.2) | async-done | bytes 10616864 | tf_op jit(solution)/shard_map/all_to_all | solution.py:39
  163.0 6.3 all-to-all-start
  169.3 12.6 fusion.64
  181.9 3.7 copy.23
  185.5 15.8 %copy.12 = bf16[144,2,16,1152]{3,1,0,2:T(2,128)(2,1)} copy(bf16[144,2,16,1152]{3,2,1,0:T(8,128)(2,1)S(1)} %bitcast.57) | data formatting | bytes 21233664 | tf_op jit(solution)/shard_map/reshape;squeeze | solution.py:30
  201.4 157.3 %all-to-all-done = bf16[144,2,16,1152]{3,1,0,2:T(2,128)(2,1)} async-done(((bf16[144,2,16,1152]{3,1,0,2:T(2,128)(2,1)}), bf16[144,2,16,1152]{3,1,0,2:T(2,128)(2,1)}, u32[]{:S(2)}, u32[]{:S(2)}) %all-to-all-start) | async-done | bytes 10616864 | tf_op jit(solution)/shard_map/all_to_all | solution.py:32
  358.7 45.5 %all-to-all-start.1 = ((bf16[144,2,16,1152]{3,1,0,2:T(2,128)(2,1)}), bf16[144,2,16,1152]{3,1,0,2:T(2,128)(2,1)}, u32[]{:S(2)}, u32[]{:S(2)}) async-start(bf16[144,2,16,1152]{3,1,0,2:T(2,128)(2,1)} %copy.12), calls=%async_computation.1 | async-start | bytes 21233664 | tf_op jit(solution)/shard_map/all_to_all | solution.py:33
  404.2 7.1 copy.25
  411.3 15.8 %copy.15 = bf16[144,2,16,1152]{3,1,0,2:T(2,128)(2,1)} copy(bf16[144,2,16,1152]{3,2,1,0:T(8,128)(2,1)S(1)} %bitcast.58) | data formatting | bytes 21233664 | tf_op jit(solution)/shard_map/reshape;squeeze | solution.py:27
  427.2 166.4 %all-to-all-done.1 = bf16[144,2,16,1152]{3,1,0,2:T(2,128)(2,1)} async-done(((bf16[144,2,16,1152]{3,1,0,2:T(2,128)(2,1)}), bf16[144,2,16,1152]{3,1,0,2:T(2,128)(2,1)}, u32[]{:S(2)}, u32[]{:S(2)}) %all-to-all-start.1) | async-done | bytes 10616864 | tf_op jit(solution)/shard_map/all_to_all | solution.py:33
  593.6 45.5 %all-to-all-start.3 = ((bf16[144,2,16,1152]{3,1,0,2:T(2,128)(2,1)}), bf16[144,2,16,1152]{3,1,0,2:T(2,128)(2,1)}, u32[]{:S(2)}, u32[]{:S(2)}) async-start(bf16[144,2,16,1152]{3,1,0,2:T(2,128)(2,1)} %copy.15), calls=%async_computation.4 | async-start | bytes 21233664 | tf_op jit(solution)/shard_map/all_to_all | solution.py:32
  639.1 0.0 all-gather.3.cloned.1.call-start
  639.1 0.1 fusion.44
  639.3 4.9 psum.42
  644.2 0.1 add_reduce_fusion.1
  644.3 0.8 fusion.46
  645.1 7.1 copy.27
  652.2 15.9 %copy.16 = bf16[144,2,16,1152]{3,1,0,2:T(2,128)(2,1)} copy(bf16[144,2,16,1152]{3,2,1,0:T(8,128)(2,1)S(1)} %bitcast.59) | data formatting | bytes 21233664 | tf_op jit(solution)/shard_map/reshape;squeeze | solution.py:30
  668.1 11.3 copy.22
  679.4 11.3 copy.24
  690.7 152.0 %all-to-all-done.3 = bf16[144,2,16,1152]{3,1,0,2:T(2,128)(2,1)} async-done(((bf16[144,2,16,1152]{3,1,0,2:T(2,128)(2,1)}), bf16[144,2,16,1152]{3,1,0,2:T(2,128)(2,1)}, u32[]{:S(2)}, u32[]{:S(2)}) %all-to-all-start.3) | async-done | bytes 10616864 | tf_op jit(solution)/shard_map/all_to_all | solution.py:32
  842.7 45.4 %all-to-all-start.4 = ((bf16[144,2,16,1152]{3,1,0,2:T(2,128)(2,1)}), bf16[144,2,16,1152]{3,1,0,2:T(2,128)(2,1)}, u32[]{:S(2)}, u32[]{:S(2)}) async-start(bf16[144,2,16,1152]{3,1,0,2:T(2,128)(2,1)} %copy.16), calls=%async_computation.5 | async-start | bytes 21233664 | tf_op jit(solution)/shard_map/all_to_all | solution.py:33
  888.1 0.2 all-reduce.3.cloned.1.call-start
  888.4 0.0 all-gather.3.cloned.1.call-done
  888.4 16.6 %fusion.11 = bf16[512,4608]{1,0:T(8,128)(2,1)} fusion(bf16[512,2304]{1,0:T(8,128)(2,1)} %all-gather.3.cloned.1.call-done, bf16[2304,2304]{1,0:T(8,128)(2,1)} %bitcast.66, bf16[2304,2304]{1,0:T(8,128)(2,1)} %bitcast.64), kind=kOutput, calls=%fused_computation.9 | convolution fusion | flops 10916462592 | bytes 28311552 | tf_op jit(solution)/shard_map/dot_general | solution.py:47
  905.0 0.0 all-reduce.3.cloned.1.call-update
  905.0 0.0 reduce-scatter.3.cloned.1.call-start
  905.1 15.6 %copy.14 = bf16[2,1152,2304]{2,1,0:T(8,128)(2,1)} copy(bf16[2,1152,2304]{1,2,0:T(8,128)(2,1)} %bitcast.5) | data formatting | bytes 21233664 | tf_op jit(solution)/shard_map/all_to_all | solution.py:39
  920.7 104.1 %all-reduce.3.cloned.1.call-done = bf16[512,4608]{1,0:T(8,128)(2,1)} async-done(((bf16[512,4608]{1,0:T(8,128)(2,1)}), bf16[512,4608]{1,0:T(8,128)(2,1)}) %all-reduce.3.cloned.1.call-update) | async-done | bytes 4718608 | tf_op jit(solution)/shard_map/psum | solution.py:52
  1024.8 3.7 convert_element_type.39
  1028.5 1.7 copy-done
  1030.2 8.3 fusion.34
  1038.5 0.0 all-gather.5.cloned.1.call-start
  1038.6 0.1 add_reduce_fusion
  1038.7 93.3 %reduce-scatter.3.cloned.1.call-done = f32[32,2304]{1,0:T(8,128)} async-done(((f32[512,2304]{1,0:T(8,128)}), f32[32,2304]{1,0:T(8,128)}) %reduce-scatter.3.cloned.1.call-update) | async-done | bytes 294928 | tf_op jit(solution)/shard_map/reduce_scatter | solution.py:54
  1132.0 1.1 multiply_reduce_fusion.1
  1133.1 4.9 psum.44
  1138.0 1.2 fusion.48
  1139.2 4.9 psum.45
  1144.2 0.8 fusion.50
  1145.0 15.3 %copy.20 = bf16[1,1152,4608]{1,2,0:T(8,128)(2,1)} copy(bf16[1,1152,4608]{2,1,0:T(8,128)(2,1)} %get-tuple-element.15) | data formatting | bytes 21233664
  1160.2 11.4 copy.26
  1171.6 7.7 all-to-all-start.5
  1179.3 0.3 all-reduce.5.cloned.1.call-start
  1179.6 11.4 copy.28
  1191.0 11.0 all-gather.5.cloned.1.call-done
  1202.0 16.7 %fusion.8 = bf16[512,4608]{1,0:T(8,128)(2,1)} fusion(bf16[512,2304]{1,0:T(8,128)(2,1)} %all-gather.5.cloned.1.call-done, bf16[2304,2304]{1,0:T(8,128)(2,1)} %bitcast.68, bf16[2304,2304]{1,0:T(8,128)(2,1)} %bitcast.65), kind=kOutput, calls=%fused_computation.8 | convolution fusion | flops 10916462592 | bytes 28311552 | tf_op jit(solution)/shard_map/dot_general | solution.py:47
  1218.7 0.0 reduce-scatter.5.cloned.1.call-start
  1218.7 128.1 %all-to-all-done.5 = bf16[1152,2,2304]{0,2,1:T(8,128)(2,1)} async-done(((bf16[1152,2,2304]{0,2,1:T(8,128)(2,1)}), bf16[1152,2,2304]{0,2,1:T(8,128)(2,1)}, u32[]{:S(2)}, u32[]{:S(2)}) %all-to-all-start.5) | async-done | bytes 10616864 | tf_op jit(solution)/shard_map/all_to_all | solution.py:39
  1346.9 15.6 %copy.18 = bf16[2,1152,2304]{2,1,0:T(8,128)(2,1)} copy(bf16[2,1152,2304]{1,2,0:T(8,128)(2,1)} %bitcast.12) | data formatting | bytes 21233664 | tf_op jit(solution)/shard_map/all_to_all | solution.py:39
  1362.5 32.4 %all-reduce.5.cloned.1.call-done = bf16[512,4608]{1,0:T(8,128)(2,1)} async-done(((bf16[512,4608]{1,0:T(8,128)(2,1)}), bf16[512,4608]{1,0:T(8,128)(2,1)}) %all-reduce.5.cloned.1.call-update) | async-done | bytes 4718608 | tf_op jit(solution)/shard_map/psum | solution.py:52
  1394.9 3.7 convert_element_type.45
  1398.6 1.7 copy-done.1
  1400.3 8.3 fusion.32
  1408.6 90.3 %reduce-scatter.5.cloned.1.call-done = f32[32,2304]{1,0:T(8,128)} async-done(((f32[512,2304]{1,0:T(8,128)}), f32[32,2304]{1,0:T(8,128)}) %reduce-scatter.5.cloned.1.call-update) | async-done | bytes 294928 | tf_op jit(solution)/shard_map/reduce_scatter | solution.py:54
  1499.0 1.1 multiply_reduce_fusion
  1500.1 4.9 psum.47
  1505.0 1.7 fusion.51
  (18 shorter events, 0.1 us)
Async XLA Ops:
  37.6 125.4 %all-to-all-start.2 = ((bf16[1152,2,2304]{0,2,1:T(8,128)(2,1)}), bf16[1152,2,2304]{0,2,1:T(8,128)(2,1)}, u32[]{:S(2)}, u32[]{:S(2)}) async-start(bf16[1152,2,2304]{0,2,1:T(8,128)(2,1)} %bitcast.55), calls=%async_computation.2 | async-start | bytes 21233664 | tf_op jit(solution)/shard_map/all_to_all | solution.py:39
  163.0 195.7 %all-to-all-start = ((bf16[144,2,16,1152]{3,1,0,2:T(2,128)(2,1)}), bf16[144,2,16,1152]{3,1,0,2:T(2,128)(2,1)}, u32[]{:S(2)}, u32[]{:S(2)}) async-start(bf16[144,2,16,1152]{3,1,0,2:T(2,128)(2,1)} %copy.11), calls=%async_computation | async-start | bytes 21233664 | tf_op jit(solution)/shard_map/all_to_all | solution.py:32
  358.7 234.9 %all-to-all-start.1 = ((bf16[144,2,16,1152]{3,1,0,2:T(2,128)(2,1)}), bf16[144,2,16,1152]{3,1,0,2:T(2,128)(2,1)}, u32[]{:S(2)}, u32[]{:S(2)}) async-start(bf16[144,2,16,1152]{3,1,0,2:T(2,128)(2,1)} %copy.12), calls=%async_computation.1 | async-start | bytes 21233664 | tf_op jit(solution)/shard_map/all_to_all | solution.py:33
  427.1 212.0 %copy-start.2 = (bf16[32,2304]{1,0:T(8,128)(2,1)S(1)}, bf16[32,2304]{1,0:T(8,128)(2,1)}, u32[]{:S(2)}) copy-start(bf16[32,2304]{1,0:T(8,128)(2,1)} %param.6) | copy-start | bytes 442372
  427.1 217.1 %copy-start.3 = (f32[2,2304]{1,0:T(2,128)S(1)}, f32[2,2304]{1,0:T(2,128)}, u32[]{:S(2)}) copy-start(f32[2,2304]{1,0:T(2,128)} %param.7) | copy-start | bytes 55300
  593.6 249.1 %all-to-all-start.3 = ((bf16[144,2,16,1152]{3,1,0,2:T(2,128)(2,1)}), bf16[144,2,16,1152]{3,1,0,2:T(2,128)(2,1)}, u32[]{:S(2)}, u32[]{:S(2)}) async-start(bf16[144,2,16,1152]{3,1,0,2:T(2,128)(2,1)} %copy.15), calls=%async_computation.4 | async-start | bytes 21233664 | tf_op jit(solution)/shard_map/all_to_all | solution.py:32
  639.1 249.3 %all-gather.3.cloned.1.call-start = ((), (), s32[]{:S(2)}) async-start(), calls=%async_computation.8 | async-start | bytes 2506752 | tf_op jit(solution)/shard_map/all_gather | solution.py:48
  842.7 328.9 %all-to-all-start.4 = ((bf16[144,2,16,1152]{3,1,0,2:T(2,128)(2,1)}), bf16[144,2,16,1152]{3,1,0,2:T(2,128)(2,1)}, u32[]{:S(2)}, u32[]{:S(2)}) async-start(bf16[144,2,16,1152]{3,1,0,2:T(2,128)(2,1)} %copy.16), calls=%async_computation.5 | async-start | bytes 21233664 | tf_op jit(solution)/shard_map/all_to_all | solution.py:33
  888.1 136.7 %all-reduce.3.cloned.1.call-start = ((), (), s32[]{:S(2)}) async-start(), calls=%async_computation.9 | async-start | bytes 9437184 | tf_op jit(solution)/shard_map/psum | solution.py:52
  905.0 227.0 %reduce-scatter.3.cloned.1.call-start = ((), (), s32[]{:S(2)}) async-start(), calls=%async_computation.10 | async-start | bytes 5013504 | tf_op jit(solution)/shard_map/reduce_scatter | solution.py:54
  1024.8 5.4 copy-start
  1030.2 8.4 copy-start.4
  1038.5 163.4 %all-gather.5.cloned.1.call-start = ((), (), s32[]{:S(2)}) async-start(), calls=%async_computation.11 | async-start | bytes 2506752 | tf_op jit(solution)/shard_map/all_gather | solution.py:48
  1171.6 175.2 %all-to-all-start.5 = ((bf16[1152,2,2304]{0,2,1:T(8,128)(2,1)}), bf16[1152,2,2304]{0,2,1:T(8,128)(2,1)}, u32[]{:S(2)}, u32[]{:S(2)}) async-start(bf16[1152,2,2304]{0,2,1:T(8,128)(2,1)} %bitcast.54), calls=%async_computation.6 | async-start | bytes 21233664 | tf_op jit(solution)/shard_map/all_to_all | solution.py:39
  1179.3 215.6 %all-reduce.5.cloned.1.call-start = ((), (), s32[]{:S(2)}) async-start(), calls=%async_computation.12 | async-start | bytes 9437184 | tf_op jit(solution)/shard_map/psum | solution.py:52
  1218.7 280.3 %reduce-scatter.5.cloned.1.call-start = ((), (), s32[]{:S(2)}) async-start(), calls=%async_computation.13 | async-start | bytes 5013504 | tf_op jit(solution)/shard_map/reduce_scatter | solution.py:54
  1394.9 5.4 copy-start.1
Sparse Core Ops, SparseCore 0:
  645.2 161.6 all-gather.2
  905.2 119.5 all-reduce.2
  1038.7 93.2 reduce-scatter.2
  1145.1 56.8 all-gather.4
  1218.8 176.0 all-reduce.4
  1408.7 90.1 reduce-scatter.4
where the time goes:
time: 1520 us; the launch traced here: 1510 us
  waiting for transfers between devices  1020 us (67%)
  local copies, waits for them, and re-layouts  237 us (16%)
  starting transfers between devices  159 us (10%)
  matrix products  49.9 us (3%)
  blocking collectives  19.7 us (1%)
    all_to_all x2, waiting for transfers between devices, on_device(): lax.all_to_all(gate_split, 'col', split_axis=2, concat_axis=0, tiled=True)  309 us
    all_to_all x2, waiting for transfers between devices, on_device(): lax.all_to_all(down_weight[layer_index], 'row', split_axis=1, concat_axis...  214 us
    reduce_scatter x2, waiting for transfers between devices, on_device(): lax.psum_scatter(jnp.dot(hidden, down_tile, preferred_element_type=jnp.fl...  184 us
    all_to_all x2, waiting for transfers between devices, on_device(): lax.all_to_all(up_split, 'col', split_axis=2, concat_axis=0, tiled=True)  166 us
    psum x2, waiting for transfers between devices, on_device(): lax.psum(partial_sums.astype(jnp.bfloat16), 'row').astype(jnp.float32)  136 us
    unnamed x20, local copies, waits for them, and re-layouts  101 us
    all_to_all x2, starting transfers between devices, on_device(): lax.all_to_all(up_split, 'col', split_axis=2, concat_axis=0, tiled=True)  90.9 us
    all_to_all x2, starting transfers between devices, on_device(): lax.all_to_all(gate_split, 'col', split_axis=2, concat_axis=0, tiled=True)  51.8 us
  transfers between devices with their start and end apart: 12, of which 10 were waited for; matrix products, arithmetic and copies ran while one was open for 17% of the time, Pallas kernels for 0%

commit v1 on v0

--- a/solution.py
+++ b/solution.py
@@ -49,7 +49,9 @@
             gate_up,
             preferred_element_type=jnp.float32,
         )
-        summed = lax.psum(partial_sums.astype(jnp.bfloat16), "row").astype(jnp.float32)
+        summed = jnp.sum(lax.all_gather(partial_sums.astype(jnp.bfloat16), "row"), axis=0).astype(
+            jnp.float32
+        )
         hidden = activate(summed, columns)
         branch = lax.psum_scatter(
             jnp.dot(hidden, down_tile, preferred_element_type=jnp.float32),

time: 1520 us -> 1570 us (1.033)
  blocking collectives: 19.7 us -> 234 us
  waiting for transfers between devices: 1020 us -> 848 us
  other arithmetic: 14.3 us -> 32.1 us
    all_to_all x0 -> x1, blocking collectives: none -> 215 us  [on_device(): lax.all_to_all(down_weight[layer_index], 'row', split_axis=1, concat_axis...]
    all_gather x2, waiting for transfers between devices: 11 us -> 176 us  [on_device(): lax.all_gather(normed, 'col', axis=0, tiled=True)]
    all_to_all x2, waiting for transfers between devices: 309 us -> 157 us  [on_device(): lax.all_to_all(gate_split, 'col', split_axis=2, concat_axis=0, tiled=True)]
    psum x2 -> x0, waiting for transfers between devices: 136 us -> none  [on_device(): lax.psum(partial_sums.astype(jnp.bfloat16), 'row').astype(jnp.float32)]
    all_to_all x2 -> x1, waiting for transfers between devices: 214 us -> 85.5 us  [on_device(): lax.all_to_all(down_weight[layer_index], 'row', split_axis=1, concat_axis...]
    all_gather x0 -> x2, waiting for transfers between devices: none -> 59.7 us  [on_device(): lax.all_gather(partial_sums.astype(jnp.bfloat16), 'row')]
    reduce_scatter x2, waiting for transfers between devices: 184 us -> 203 us  [on_device(): lax.psum_scatter(jnp.dot(hidden, down_tile, preferred_element_type=jnp.fl...]
    reduce_sum x0 -> x2, other arithmetic: none -> 17.8 us  [on_device(): jnp.sum(lax.all_gather(partial_sums.astype(jnp.bfloat16), 'row'), axis=0)]
  transfers between devices with their start and end apart: 12 -> 11, of which waited for: 10 -> 8; matrix products, arithmetic and copies ran while one was open for 17% -> 16% of each run, Pallas kernels for 0% -> 0%
where the time goes in v1:
time: 1570 us; the launch traced here: 1560 us
  waiting for transfers between devices  848 us (54%)
  local copies, waits for them, and re-layouts  237 us (15%)
  blocking collectives  234 us (15%)
  starting transfers between devices  148 us (9%)
  matrix products  49.8 us (3%)
  other arithmetic  32.1 us (2%)
    all_to_all x1, blocking collectives, on_device(): lax.all_to_all(down_weight[layer_index], 'row', split_axis=1, concat_axis...  215 us
    reduce_scatter x2, waiting for transfers between devices, on_device(): lax.psum_scatter(jnp.dot(hidden, down_tile, preferred_element_type=jnp.fl...  203 us
    all_gather x2, waiting for transfers between devices, on_device(): lax.all_gather(normed, 'col', axis=0, tiled=True)  176 us
    all_to_all x2, waiting for transfers between devices, on_device(): lax.all_to_all(up_split, 'col', split_axis=2, concat_axis=0, tiled=True)  166 us
    all_to_all x2, waiting for transfers between devices, on_device(): lax.all_to_all(gate_split, 'col', split_axis=2, concat_axis=0, tiled=True)  157 us
    unnamed x20, local copies, waits for them, and re-layouts  101 us
    all_to_all x2, starting transfers between devices, on_device(): lax.all_to_all(up_split, 'col', split_axis=2, concat_axis=0, tiled=True)  87.1 us
    all_to_all x1, waiting for transfers between devices, on_device(): lax.all_to_all(down_weight[layer_index], 'row', split_axis=1, concat_axis...  85.5 us
  transfers between devices with their start and end apart: 11, of which 8 were waited for; matrix products, arithmetic and copies ran while one was open for 16% of the time, Pallas kernels for 0%

profile of v1, /device:TPU:0, one launch (start us, length us, event | category | flops | bytes accessed | tf_op | source)
XLA Modules:
  0.0 1562.1 jit_solution(11301309608102874984)
XLA Ops:
  6.5 15.8 %fusion.65 = (bf16[1,1152,4608]{2,1,0:T(8,128)(2,1)}, bf16[1,1152,4608]{2,1,0:T(8,128)(2,1)}) fusion(bf16[2,1152,4608]{2,1,0:T(8,128)(2,1)} %param.11), kind=kLoop, calls=%fused_computation.76 | loop fusion | bytes 42467328 | tf_op jit(solution)/shard_map/slice | solution.py:40
  22.3 15.2 copy.19
  37.6 7.8 all-to-all-start.2
  45.4 12.6 fusion.63
  58.0 3.7 copy.21
  61.7 15.8 %copy.11 = bf16[144,2,16,1152]{3,1,0,2:T(2,128)(2,1)} copy(bf16[144,2,16,1152]{3,2,1,0:T(8,128)(2,1)S(1)} %bitcast.57) | data formatting | bytes 21233664 | tf_op jit(solution)/shard_map/reshape;squeeze | solution.py:27
  77.5 85.5 %all-to-all-done.2 = bf16[1152,2,2304]{0,2,1:T(8,128)(2,1)} async-done(((bf16[1152,2,2304]{0,2,1:T(8,128)(2,1)}), bf16[1152,2,2304]{0,2,1:T(8,128)(2,1)}, u32[]{:S(2)}, u32[]{:S(2)}) %all-to-all-start.2) | async-done | bytes 10616864 | tf_op jit(solution)/shard_map/all_to_all | solution.py:39
  163.0 6.3 all-to-all-start
  169.3 12.6 fusion.64
  181.9 3.7 copy.23
  185.5 15.8 %copy.12 = bf16[144,2,16,1152]{3,1,0,2:T(2,128)(2,1)} copy(bf16[144,2,16,1152]{3,2,1,0:T(8,128)(2,1)S(1)} %bitcast.58) | data formatting | bytes 21233664 | tf_op jit(solution)/shard_map/reshape;squeeze | solution.py:30
  201.4 157.3 %all-to-all-done = bf16[144,2,16,1152]{3,1,0,2:T(2,128)(2,1)} async-done(((bf16[144,2,16,1152]{3,1,0,2:T(2,128)(2,1)}), bf16[144,2,16,1152]{3,1,0,2:T(2,128)(2,1)}, u32[]{:S(2)}, u32[]{:S(2)}) %all-to-all-start) | async-done | bytes 10616864 | tf_op jit(solution)/shard_map/all_to_all | solution.py:32
  358.7 45.5 %all-to-all-start.1 = ((bf16[144,2,16,1152]{3,1,0,2:T(2,128)(2,1)}), bf16[144,2,16,1152]{3,1,0,2:T(2,128)(2,1)}, u32[]{:S(2)}, u32[]{:S(2)}) async-start(bf16[144,2,16,1152]{3,1,0,2:T(2,128)(2,1)} %copy.12), calls=%async_computation.1 | async-start | bytes 21233664 | tf_op jit(solution)/shard_map/all_to_all | solution.py:33
  404.2 7.1 copy.25
  411.3 15.8 %copy.15 = bf16[144,2,16,1152]{3,1,0,2:T(2,128)(2,1)} copy(bf16[144,2,16,1152]{3,2,1,0:T(8,128)(2,1)S(1)} %bitcast.59) | data formatting | bytes 21233664 | tf_op jit(solution)/shard_map/reshape;squeeze | solution.py:27
  427.2 166.4 %all-to-all-done.1 = bf16[144,2,16,1152]{3,1,0,2:T(2,128)(2,1)} async-done(((bf16[144,2,16,1152]{3,1,0,2:T(2,128)(2,1)}), bf16[144,2,16,1152]{3,1,0,2:T(2,128)(2,1)}, u32[]{:S(2)}, u32[]{:S(2)}) %all-to-all-start.1) | async-done | bytes 10616864 | tf_op jit(solution)/shard_map/all_to_all | solution.py:33
  593.6 45.5 %all-to-all-start.3 = ((bf16[144,2,16,1152]{3,1,0,2:T(2,128)(2,1)}), bf16[144,2,16,1152]{3,1,0,2:T(2,128)(2,1)}, u32[]{:S(2)}, u32[]{:S(2)}) async-start(bf16[144,2,16,1152]{3,1,0,2:T(2,128)(2,1)} %copy.15), calls=%async_computation.4 | async-start | bytes 21233664 | tf_op jit(solution)/shard_map/all_to_all | solution.py:32
  639.1 0.0 all-gather.7.cloned.1.call-start
  639.1 0.1 fusion.44
  639.3 4.9 psum.28
  644.2 0.1 add_reduce_fusion.1
  644.3 0.8 fusion.46
  645.0 0.0 all-gather.7.cloned.1.call-update
  645.1 0.2 all-gather.11.cloned.1.call-start
  645.3 11.4 copy.22
  656.7 11.3 copy.24
  668.0 138.9 %all-gather.7.cloned.1.call-done = bf16[512,2304]{1,0:T(8,128)(2,1)} async-done(((bf16[32,2304]{1,0:T(8,128)(2,1)}), bf16[512,2304]{1,0:T(8,128)(2,1)}) %all-gather.7.cloned.1.call-update) | async-done | bytes 2359312 | tf_op jit(solution)/shard_map/all_gather | solution.py:48
  806.9 16.6 %fusion.11 = bf16[512,4608]{1,0:T(8,128)(2,1)} fusion(bf16[512,2304]{1,0:T(8,128)(2,1)} %all-gather.7.cloned.1.call-done, bf16[2304,2304]{1,0:T(8,128)(2,1)} %bitcast.71, bf16[2304,2304]{1,0:T(8,128)(2,1)} %bitcast.70), kind=kOutput, calls=%fused_computation.9 | convolution fusion | flops 10916462592 | bytes 28311552 | tf_op jit(solution)/shard_map/dot_general | solution.py:47
  823.5 0.0 all-gather.11.cloned.1.call-update
  823.5 7.1 copy.27
  830.6 15.9 %copy.16 = bf16[144,2,16,1152]{3,1,0,2:T(2,128)(2,1)} copy(bf16[144,2,16,1152]{3,2,1,0:T(8,128)(2,1)S(1)} %bitcast.60) | data formatting | bytes 21233664 | tf_op jit(solution)/shard_map/reshape;squeeze | solution.py:30
  846.5 41.6 %all-to-all-start.4 = ((bf16[144,2,16,1152]{3,1,0,2:T(2,128)(2,1)}), bf16[144,2,16,1152]{3,1,0,2:T(2,128)(2,1)}, u32[]{:S(2)}, u32[]{:S(2)}) async-start(bf16[144,2,16,1152]{3,1,0,2:T(2,128)(2,1)} %copy.16), calls=%async_computation.5 | async-start | bytes 21233664 | tf_op jit(solution)/shard_map/all_to_all | solution.py:33
  888.1 0.3 reduce-scatter.3.cloned.1.call-start
  888.4 15.6 copy.14
  904.0 59.7 %all-gather.11.cloned.1.call-done = bf16[1024,4608]{1,0:T(8,128)(2,1)} async-done(((bf16[512,4608]{1,0:T(8,128)(2,1)}), bf16[1024,4608]{1,0:T(8,128)(2,1)}) %all-gather.11.cloned.1.call-update) | async-done | bytes 9437200 | tf_op jit(solution)/shard_map/all_gather | solution.py:52
  963.7 8.8 reduce_sum.61
  972.5 3.7 convert_element_type.43
  976.2 1.7 copy-done.1
  978.0 8.3 fusion.34
  986.3 0.0 all-gather.9.cloned.1.call-start
  986.3 0.1 add_reduce_fusion
  986.4 126.9 %reduce-scatter.3.cloned.1.call-done = f32[32,2304]{1,0:T(8,128)} async-done(((f32[512,2304]{1,0:T(8,128)}), f32[32,2304]{1,0:T(8,128)}) %reduce-scatter.3.cloned.1.call-update) | async-done | bytes 294928 | tf_op jit(solution)/shard_map/reduce_scatter | solution.py:56
  1113.3 1.1 multiply_reduce_fusion.1
  1114.3 4.9 psum.29
  1119.3 1.2 fusion.48
  1120.5 4.9 psum.30
  1125.4 0.8 fusion.50
  1126.2 0.3 all-gather.13.cloned.1.call-start
  1126.5 11.4 copy.26
  1137.9 11.3 copy.28
  1149.2 37.2 %all-gather.9.cloned.1.call-done = bf16[512,2304]{1,0:T(8,128)(2,1)} async-done(((bf16[32,2304]{1,0:T(8,128)(2,1)}), bf16[512,2304]{1,0:T(8,128)(2,1)}) %all-gather.9.cloned.1.call-update) | async-done | bytes 2359312 | tf_op jit(solution)/shard_map/all_gather | solution.py:48
  1186.5 16.6 %fusion.8 = bf16[512,4608]{1,0:T(8,128)(2,1)} fusion(bf16[512,2304]{1,0:T(8,128)(2,1)} %all-gather.9.cloned.1.call-done, bf16[2304,2304]{1,0:T(8,128)(2,1)} %bitcast.72, bf16[2304,2304]{1,0:T(8,128)(2,1)} %bitcast.67), kind=kOutput, calls=%fused_computation.8 | convolution fusion | flops 10916462592 | bytes 28311552 | tf_op jit(solution)/shard_map/dot_general | solution.py:47
  1203.1 0.0 reduce-scatter.5.cloned.1.call-start
  1203.2 15.7 %copy.20 = bf16[1,1152,4608]{1,2,0:T(8,128)(2,1)} copy(bf16[1,1152,4608]{2,1,0:T(8,128)(2,1)} %get-tuple-element.15) | data formatting | bytes 21233664
  1218.9 214.7 %all_to_all.98 = bf16[1152,2,2304]{0,2,1:T(8,128)(2,1)} all-to-all(bf16[1152,2,2304]{0,2,1:T(8,128)(2,1)} %bitcast.61), channel_id=1, replica_groups=mesh['row'=2,'col'=16] {'row'}, dimensions={1} | all-to-all | bytes 21233664 | tf_op jit(solution)/shard_map/all_to_all | solution.py:39
  1433.6 15.5 copy.18
  1449.1 8.9 reduce_sum.64
  1458.0 3.7 convert_element_type.49
  1461.8 1.7 copy-done
  1463.5 8.3 fusion.32
  1471.8 75.7 %reduce-scatter.5.cloned.1.call-done = f32[32,2304]{1,0:T(8,128)} async-done(((f32[512,2304]{1,0:T(8,128)}), f32[32,2304]{1,0:T(8,128)}) %reduce-scatter.5.cloned.1.call-update) | async-done | bytes 294928 | tf_op jit(solution)/shard_map/reduce_scatter | solution.py:56
  1547.5 1.1 multiply_reduce_fusion
  1548.6 4.9 psum.31
  1553.5 1.7 fusion.51
  (19 shorter events, 0.1 us)
Async XLA Ops:
  37.6 125.4 %all-to-all-start.2 = ((bf16[1152,2,2304]{0,2,1:T(8,128)(2,1)}), bf16[1152,2,2304]{0,2,1:T(8,128)(2,1)}, u32[]{:S(2)}, u32[]{:S(2)}) async-start(bf16[1152,2,2304]{0,2,1:T(8,128)(2,1)} %bitcast.56), calls=%async_computation.2 | async-start | bytes 21233664 | tf_op jit(solution)/shard_map/all_to_all | solution.py:39
  163.0 195.7 %all-to-all-start = ((bf16[144,2,16,1152]{3,1,0,2:T(2,128)(2,1)}), bf16[144,2,16,1152]{3,1,0,2:T(2,128)(2,1)}, u32[]{:S(2)}, u32[]{:S(2)}) async-start(bf16[144,2,16,1152]{3,1,0,2:T(2,128)(2,1)} %copy.11), calls=%async_computation | async-start | bytes 21233664 | tf_op jit(solution)/shard_map/all_to_all | solution.py:32
  358.7 234.9 %all-to-all-start.1 = ((bf16[144,2,16,1152]{3,1,0,2:T(2,128)(2,1)}), bf16[144,2,16,1152]{3,1,0,2:T(2,128)(2,1)}, u32[]{:S(2)}, u32[]{:S(2)}) async-start(bf16[144,2,16,1152]{3,1,0,2:T(2,128)(2,1)} %copy.12), calls=%async_computation.1 | async-start | bytes 21233664 | tf_op jit(solution)/shard_map/all_to_all | solution.py:33
  427.2 212.0 %copy-start.2 = (bf16[32,2304]{1,0:T(8,128)(2,1)S(1)}, bf16[32,2304]{1,0:T(8,128)(2,1)}, u32[]{:S(2)}) copy-start(bf16[32,2304]{1,0:T(8,128)(2,1)} %param.6) | copy-start | bytes 442372
  427.2 217.0 %copy-start.3 = (f32[2,2304]{1,0:T(2,128)S(1)}, f32[2,2304]{1,0:T(2,128)}, u32[]{:S(2)}) copy-start(f32[2,2304]{1,0:T(2,128)} %param.7) | copy-start | bytes 55300
  593.6 252.9 %all-to-all-start.3 = ((bf16[144,2,16,1152]{3,1,0,2:T(2,128)(2,1)}), bf16[144,2,16,1152]{3,1,0,2:T(2,128)(2,1)}, u32[]{:S(2)}, u32[]{:S(2)}) async-start(bf16[144,2,16,1152]{3,1,0,2:T(2,128)(2,1)} %copy.15), calls=%async_computation.4 | async-start | bytes 21233664 | tf_op jit(solution)/shard_map/all_to_all | solution.py:32
  639.1 167.8 %all-gather.7.cloned.1.call-start = ((), (), s32[]{:S(2)}) async-start(), calls=%async_computation.8 | async-start | bytes 2506752 | tf_op jit(solution)/shard_map/all_gather | solution.py:48
  645.1 318.6 %all-gather.11.cloned.1.call-start = ((), (), s32[]{:S(2)}) async-start(), calls=%async_computation.12 | async-start | bytes 14155776 | tf_op jit(solution)/shard_map/all_gather | solution.py:52
  846.5 291.4 %all-to-all-start.4 = ((bf16[144,2,16,1152]{3,1,0,2:T(2,128)(2,1)}), bf16[144,2,16,1152]{3,1,0,2:T(2,128)(2,1)}, u32[]{:S(2)}, u32[]{:S(2)}) async-start(bf16[144,2,16,1152]{3,1,0,2:T(2,128)(2,1)} %copy.16), calls=%async_computation.5 | async-start | bytes 21233664 | tf_op jit(solution)/shard_map/all_to_all | solution.py:33
  888.1 225.1 %reduce-scatter.3.cloned.1.call-start = ((), (), s32[]{:S(2)}) async-start(), calls=%async_computation.9 | async-start | bytes 5013504 | tf_op jit(solution)/shard_map/reduce_scatter | solution.py:56
  972.5 5.4 copy-start.1
  977.9 8.4 copy-start.4
  986.3 200.2 %all-gather.9.cloned.1.call-start = ((), (), s32[]{:S(2)}) async-start(), calls=%async_computation.10 | async-start | bytes 2506752 | tf_op jit(solution)/shard_map/all_gather | solution.py:48
  1126.2 322.9 %all-gather.13.cloned.1.call-start = ((), (), s32[]{:S(2)}) async-start(), calls=%async_computation.13 | async-start | bytes 14155776 | tf_op jit(solution)/shard_map/all_gather | solution.py:52
  1203.1 344.4 %reduce-scatter.5.cloned.1.call-start = ((), (), s32[]{:S(2)}) async-start(), calls=%async_computation.11 | async-start | bytes 5013504 | tf_op jit(solution)/shard_map/reduce_scatter | solution.py:56
  1458.0 5.4 copy-start
Sparse Core Ops, SparseCore 0:
  645.2 161.6 all-gather.6
  823.6 139.9 all-gather.10
  986.4 126.8 reduce-scatter.2
  1126.3 60.0 all-gather.8
  1203.3 201.5 all-gather.12
  1471.9 75.5 reduce-scatter.4
